TPU v7x, 32 devices: a whole 2x2x4 slice. The times are simulated.
32 devices in a mesh: area: 8 (over y, x, core), rank: 4 (over z).
Axes of the slice: x: 2, y: 2, z: 4, core: 2. Of those that a mesh axis runs over, the one named last changes fastest.
Arguments:
- initial_bits: int32 [2, 48, 128], P(None, None, ('area', 'rank')), may hold values from -2147483648 to 2147483646
- membrane: float32 [48, 4096], P(None, ('area', 'rank')), may hold values from -100 to 200
- drive: int32 [4096], P(('area', 'rank')), may hold values from 0 to 47
- leak_shift: int32 [4096], P(('area', 'rank')), may hold values from 2 to 5
- weights: bfloat16 [32, 128, 128, 128], P(('area', 'rank')), may hold values from -3 to 3, as said below
- pre_block: int32 [32, 128], P(('area', 'rank')), may hold values from 0 to 31
- block_mask: int32 [32, 128], P(('area', 'rank')), may hold values 0 or 1
- delay: int32 [32, 128], P(('area', 'rank')), may hold values from 2 to 5
- area_of_block: int32 [32, 1], replicated, may hold values from 0 to 31
Outputs:
- final_membrane: float32 [48, 4096], P(None, ('area', 'rank'))
- area_rates: float32 [10, 32], replicated
Inputs may be any that keep to these rules, and one draw needn't show every extreme that they name: weights hold whole numbers. `area_of_block`: every area holds at least one block.
All inputs are finite; a program needn't handle non-finite values. No bound on the sum of `block_mask` on one device may be relied on, other than what follows from the above.
Results may differ from a plain program's by a relative error of at most 0.0003.
Values sent between devices are 32-bit elements; how exact they have to be, the bound alone decides.
A program may use at most 128 MiB of HBM per device.

v0:
```python
import functools

import jax
import jax.numpy as jnp
from jax import lax
from jax.experimental import pallas as pl
from jax.experimental.pallas import tpu as pltpu
from jax.sharding import PartitionSpec as P

AREAS = 32
DMIN = 2
NDELAY = 4
STEPS = 10
DMAX = DMIN + NDELAY - 1
INTERVALS = STEPS // DMIN
SPAN = STEPS + DMAX - DMIN
THRESHOLD = 200.0
GROUP = 8
MESH = pl.DeviceIdType.MESH


def pack(spikes):
    rows = spikes.shape[0] // 8
    word = spikes[0:8]
    for j in range(1, rows):
        word = word | (spikes[8 * j : 8 * j + 8] << j)
    return word[0:4] | (word[4:8] << rows)


def unpack(word, rows):
    word = jnp.concatenate([word, word >> rows], axis=0)
    parts = [(word & (1 << j)) != 0 for j in range(rows)]
    parts = [jnp.where(p, 1.0, 0.0) for p in parts]
    return jnp.concatenate(parts, axis=0).astype(jnp.bfloat16)


def kernel(
    sizes,
    pre_ref,
    mask_ref,
    delay_ref,
    area_ref,
    bits_ref,
    membrane_ref,
    drive_ref,
    leak_ref,
    weights_hbm,
    voltage_ref,
    rates_ref,
    weights_ref,
    history,
    outbox,
    inbox,
    count_out,
    count_in,
    base_ref,
    stride_ref,
    weight_sem,
    send_sem,
    recv_sem,
):
    areas_axis, ranks = sizes
    n = areas_axis * ranks
    me = lax.axis_index("area") * ranks + lax.axis_index("rank")
    trials, block = membrane_ref.shape
    slots = pre_ref.shape[1]
    pair = DMIN * trials
    rows = pair // 8

    load = pltpu.make_async_copy(weights_hbm, weights_ref, weight_sem)
    load.start()

    def coords(j):
        other = lax.rem(me + j, n)
        return (other // ranks, lax.rem(other, ranks))

    barrier = pltpu.get_barrier_semaphore()

    @pl.loop(1, n)
    def _(j):
        pl.semaphore_signal(barrier, inc=1, device_id=coords(j), device_id_type=MESH)

    lane = lax.broadcasted_iota(jnp.int32, (trials, block), 1)
    start = []
    for offset in range(DMIN):
        words = bits_ref[offset]
        spread = jnp.broadcast_to(words[:, 0:1], (trials, block))
        for w in range(1, block // 32):
            spread = jnp.where(lane // 32 == w, words[:, w : w + 1], spread)
        start.append((spread >> (lane % 32)) & 1)
    word = pack(jnp.concatenate(start, axis=0))

    def send(interval, word):
        outbox[interval] = word
        inbox[interval, me] = word

        @pl.loop(1, n)
        def _(j):
            pltpu.make_async_remote_copy(
                src_ref=outbox.at[interval],
                dst_ref=inbox.at[interval, me],
                send_sem=send_sem.at[interval],
                recv_sem=recv_sem.at[interval],
                device_id=coords(j),
                device_id_type=MESH,
            ).start()

    def wait(box, sem):
        region = box.at[pl.ds(0, n - 1)]
        pltpu.make_async_copy(region, region, sem).wait()

    pl.semaphore_wait(barrier, n - 1)
    send(0, word)

    @pl.loop(0, slots)
    def _(k):
        on = mask_ref[0, k]
        base_ref[k] = on * (pre_ref[0, k] * SPAN + (DMAX - delay_ref[0, k]))
        stride_ref[k] = on * DMIN

    early = DMAX - DMIN
    blank = jnp.zeros((trials, block), jnp.bfloat16)

    @pl.loop(0, n)
    def _(b):
        for s in range(early):
            history[b * SPAN + s] = blank

    scale = 1.0 / jnp.left_shift(jnp.ones_like(leak_ref[...]), leak_ref[...]).astype(jnp.float32)
    push = drive_ref[...].astype(jnp.float32)
    voltage = jnp.floor(membrane_ref[...])
    count_lane = lax.broadcasted_iota(jnp.int32, (1, block), 1)
    counts = jnp.zeros((1, block), jnp.float32)
    area_row = lax.broadcasted_iota(jnp.int32, (AREAS, block), 0)

    def tally(b, total):
        return total + jnp.where(area_row == area_ref[0, b], 1.0, 0.0)

    members = lax.fori_loop(0, n, tally, jnp.zeros((AREAS, block), jnp.float32))

    for interval in range(INTERVALS):
        wait(inbox.at[interval], recv_sem.at[interval])
        at = early + interval * DMIN

        @pl.loop(0, n, unroll=4)
        def _(b):
            spikes = unpack(inbox[interval, b], rows)
            for offset in range(DMIN):
                history[b * SPAN + at + offset] = spikes[offset * trials : (offset + 1) * trials]

        if interval == 0:
            load.wait()

        def multiply(g, total):
            picked = []
            for j in range(GROUP):
                k = g * GROUP + j
                spot = base_ref[k] + stride_ref[k] * interval
                picked.append(
                    jnp.concatenate([history[spot + s] for s in range(DMIN)], axis=0)
                )
            depth = GROUP * block
            tile = weights_ref[pl.ds(pl.multiple_of(g * depth, depth), depth), :]
            return total + jnp.dot(
                jnp.concatenate(picked, axis=1), tile, preferred_element_type=jnp.float32
            )

        current = lax.fori_loop(
            0, slots // GROUP, multiply, jnp.zeros((pair, block), jnp.float32)
        )
        fired = []
        for offset in range(DMIN):
            arrived = current[offset * trials : (offset + 1) * trials]
            voltage = voltage - jnp.floor(voltage * scale) + arrived + push
            flag = voltage >= THRESHOLD
            voltage = jnp.where(flag, 0.0, jnp.maximum(voltage, -THRESHOLD))
            fired.append(flag)
        if interval < INTERVALS - 1:
            send(interval + 1, pack(jnp.concatenate([f.astype(jnp.int32) for f in fired], axis=0)))
        for offset in range(DMIN):
            ones = jnp.sum(jnp.where(fired[offset], 1.0, 0.0), axis=0, keepdims=True)
            number = jnp.sum(ones, axis=1, keepdims=True)
            counts = jnp.where(count_lane == interval * DMIN + offset, number, counts)

    count_out[...] = counts
    count_in[me] = counts

    @pl.loop(1, n)
    def _(j):
        pltpu.make_async_remote_copy(
            src_ref=count_out,
            dst_ref=count_in.at[me],
            send_sem=send_sem.at[INTERVALS],
            recv_sem=recv_sem.at[INTERVALS],
            device_id=coords(j),
            device_id_type=MESH,
        ).start()

    voltage_ref[...] = voltage
    for interval in range(INTERVALS):
        wait(inbox.at[interval], send_sem.at[interval])
    wait(count_in, send_sem.at[INTERVALS])
    wait(count_in, recv_sem.at[INTERVALS])

    def gather(b, total):
        return total + jnp.where(area_row == area_ref[0, b], count_in[b], 0.0)

    spikes = lax.fori_loop(0, n, gather, jnp.zeros((AREAS, block), jnp.float32), unroll=4)
    rates = spikes / (members * (trials * block))
    rates_ref[...] = jnp.transpose(rates)[0:STEPS]


def solution(mesh):
    sizes = (mesh.shape["area"], mesh.shape["rank"])
    n = sizes[0] * sizes[1]

    def on_device(
        initial_bits, membrane, drive, leak_shift, weights, pre_block, block_mask, delay, area_of_block
    ):
        _, slots, block, width = weights.shape
        trials = membrane.shape[0]
        assert weights.shape[0] == 1 and area_of_block.shape[0] == n
        smem = pl.BlockSpec(memory_space=pltpu.SMEM)
        vmem = pl.BlockSpec(memory_space=pltpu.VMEM)
        return pl.pallas_call(
            functools.partial(kernel, sizes),
            out_shape=(
                jax.ShapeDtypeStruct((trials, block), jnp.float32),
                jax.ShapeDtypeStruct((STEPS, AREAS), jnp.float32),
            ),
            in_specs=[smem] * 4 + [vmem] * 4 + [pl.BlockSpec(memory_space=pl.ANY)],
            out_specs=(vmem, vmem),
            scratch_shapes=[
                pltpu.VMEM((slots * block, width), jnp.bfloat16),
                pltpu.VMEM((n * SPAN, trials, block), jnp.bfloat16),
                pltpu.VMEM((INTERVALS, 4, block), jnp.int32),
                pltpu.VMEM((INTERVALS, n, 4, block), jnp.int32),
                pltpu.VMEM((1, block), jnp.float32),
                pltpu.VMEM((n, 1, block), jnp.float32),
                pltpu.SMEM((slots,), jnp.int32),
                pltpu.SMEM((slots,), jnp.int32),
                pltpu.SemaphoreType.DMA,
                pltpu.SemaphoreType.DMA((INTERVALS + 1,)),
                pltpu.SemaphoreType.DMA((INTERVALS + 1,)),
            ],
            compiler_params=pltpu.CompilerParams(
                collective_id=0, has_side_effects=True, vmem_limit_bytes=60 * 1024 * 1024
            ),
            name="cortex_window",
        )(
            pre_block,
            block_mask,
            delay,
            area_of_block.reshape(1, -1),
            initial_bits,
            membrane,
            drive.reshape(1, -1),
            leak_shift.reshape(1, -1),
            weights.reshape(slots * block, width),
        )

    both = ("area", "rank")
    in_specs = (
        P(None, None, both),
        P(None, both),
        P(both),
        P(both),
        P(both, None, None, None),
        P(both, None),
        P(both, None),
        P(both, None),
        P(),
    )
    return jax.shard_map(
        on_device, mesh=mesh, in_specs=in_specs, out_specs=(P(None, both), P()), check_vma=False
    )
```

profile of v0, /device:TPU:0, one launch (start us, length us, event | category | flops | bytes accessed | tf_op | source)
XLA Modules:
  0.0 59.2 jit_solution(3652553702691829436)
XLA Ops:
  0.6 1.4 %copy.11.bits_ref = s32[2,48,4]{2,1,0:T(8,128)} copy(s32[2,48,4]{1,2,0:T(4,128)} %param.9) | data formatting | bytes 3072 | tf_op args[0]
  2.0 54.5 %cortex_window.1 = (f32[48,128]{1,0:T(8,128)}, f32[10,32]{1,0:T(8,128)}) custom-call(s32[1,128]{1,0:T(1,128)} %pre_ref.1, s32[1,128]{1,0:T(1,128)} %mask_ref.1, s32[1,128]{1,0:T(1,128)} %delay_ref.1, s32[1,32]{1,0:T(1,128)} %bitcast.5, s32[2,48,4]{2,1,0:T(8,128)} %copy.11.bits_ref, f32[48,128]{1,0:T(8,128)} %membrane_ref.1, s32[1,128]{1,0:T(1,128)} %bitcast.6, ...), custom_call_target="tpu_custom_call" | custom-call | tf_op jit(solution)/shard_map/cortex_window/pallas_call | solution.py:225
  56.5 1.3 %copy.14 = f32[48,128]{1,0:T(8,128)} copy(f32[48,128]{1,0:T(8,128)} %get-tuple-element.4) | data formatting | bytes 49152
  57.9 1.3 %copy.15 = f32[10,32]{1,0:T(8,128)} copy(f32[10,32]{1,0:T(8,128)} %get-tuple-element.5) | data formatting | bytes 2560
where the time goes:
time: 59.5 us; the launch traced here: 59.2 us
  Pallas kernels  54.5 us (92%)
  local copies, waits for them, and re-layouts  4.04 us (7%)
  between operations  0.64 us (1%)
    pallas_call x1, Pallas kernels, on_device(): pl.pallas_call(functools.partial(kernel, sizes), out_shape=(jax.ShapeDtyp...  54.5 us
    unnamed x3, local copies, waits for them, and re-layouts  4.04 us

commit v1 on v0

--- a/solution.py
+++ b/solution.py
@@ -15,7 +15,7 @@
 INTERVALS = STEPS // DMIN
 SPAN = STEPS + DMAX - DMIN
 THRESHOLD = 200.0
-GROUP = 8
+GROUP = 64
 MESH = pl.DeviceIdType.MESH
 
 
@@ -55,6 +55,7 @@
     count_in,
     base_ref,
     stride_ref,
+    stage,
     weight_sem,
     send_sem,
     recv_sem,
@@ -82,8 +83,13 @@
 
     lane = lax.broadcasted_iota(jnp.int32, (trials, block), 1)
     start = []
+    per = bits_ref.shape[1]
+    stage[...] = jnp.zeros_like(stage)
     for offset in range(DMIN):
-        words = bits_ref[offset]
+        stage[offset * per : (offset + 1) * per, 0:trials] = bits_ref[offset]
+    turned = jnp.transpose(stage[...])[0:trials]
+    for offset in range(DMIN):
+        words = turned[:, offset * per : (offset + 1) * per]
         spread = jnp.broadcast_to(words[:, 0:1], (trials, block))
         for w in range(1, block // 32):
             spread = jnp.where(lane // 32 == w, words[:, w : w + 1], spread)
@@ -210,6 +216,11 @@
     rates_ref[...] = jnp.transpose(rates)[0:STEPS]
 
 
+def hand_over(voltage_in, rates_in, voltage_ref, rates_ref):
+    voltage_ref[...] = voltage_in[...]
+    rates_ref[...] = rates_in[...]
+
+
 def solution(mesh):
     sizes = (mesh.shape["area"], mesh.shape["rank"])
     n = sizes[0] * sizes[1]
@@ -222,7 +233,7 @@
         assert weights.shape[0] == 1 and area_of_block.shape[0] == n
         smem = pl.BlockSpec(memory_space=pltpu.SMEM)
         vmem = pl.BlockSpec(memory_space=pltpu.VMEM)
-        return pl.pallas_call(
+        voltage, rates = pl.pallas_call(
             functools.partial(kernel, sizes),
             out_shape=(
                 jax.ShapeDtypeStruct((trials, block), jnp.float32),
@@ -239,6 +250,7 @@
                 pltpu.VMEM((n, 1, block), jnp.float32),
                 pltpu.SMEM((slots,), jnp.int32),
                 pltpu.SMEM((slots,), jnp.int32),
+                pltpu.VMEM((DMIN * (block // 32), block), jnp.int32),
                 pltpu.SemaphoreType.DMA,
                 pltpu.SemaphoreType.DMA((INTERVALS + 1,)),
                 pltpu.SemaphoreType.DMA((INTERVALS + 1,)),
@@ -252,12 +264,22 @@
             block_mask,
             delay,
             area_of_block.reshape(1, -1),
-            initial_bits,
+            initial_bits.transpose(0, 2, 1),
             membrane,
             drive.reshape(1, -1),
             leak_shift.reshape(1, -1),
             weights.reshape(slots * block, width),
         )
+        return pl.pallas_call(
+            hand_over,
+            out_shape=(
+                jax.ShapeDtypeStruct(voltage.shape, voltage.dtype),
+                jax.ShapeDtypeStruct(rates.shape, rates.dtype),
+            ),
+            in_specs=[vmem] * 2,
+            out_specs=(vmem, vmem),
+            name="hand_over",
+        )(voltage, rates)
 
     both = ("area", "rank")
     in_specs = (

time: 59.5 us -> 46.7 us (0.78)
  Pallas kernels: 54.5 us -> 45.8 us
  local copies, waits for them, and re-layouts: 4.04 us -> 0 us
    pallas_call x1, Pallas kernels: 54.5 us -> 44.5 us  [on_device(): pl.pallas_call(functools.partial(kernel, sizes), out_shape=(jax.ShapeDtyp...]
    unnamed x3 -> x0, local copies, waits for them, and re-layouts: 4.04 us -> none
    pallas_call x0 -> x1, Pallas kernels: none -> 1.35 us  [on_device(): pl.pallas_call(hand_over, out_shape=(jax.ShapeDtypeStruct(voltage.shape,...]
where the time goes in v1:
time: 46.7 us; the launch traced here: 46.5 us
  Pallas kernels  45.8 us (98%)
  between operations  0.64 us (1%)
    pallas_call x1, Pallas kernels, on_device(): pl.pallas_call(functools.partial(kernel, sizes), out_shape=(jax.ShapeDtyp...  44.5 us
    pallas_call x1, Pallas kernels, on_device(): pl.pallas_call(hand_over, out_shape=(jax.ShapeDtypeStruct(voltage.shape,...  1.35 us

profile of v1, /device:TPU:0, one launch (start us, length us, event | category | flops | bytes accessed | tf_op | source)
XLA Modules:
  0.0 46.5 jit_solution(1695075959495085224)
XLA Ops:
  0.6 44.5 %cortex_window.1 = (f32[48,128]{1,0:T(8,128)}, f32[10,32]{1,0:T(8,128)}) custom-call(s32[1,128]{1,0:T(1,128)} %pre_ref.1, s32[1,128]{1,0:T(1,128)} %mask_ref.1, s32[1,128]{1,0:T(1,128)} %delay_ref.1, s32[1,32]{1,0:T(1,128)} %bitcast.7, s32[2,4,48]{2,1,0:T(4,128)} %bitcast.6, f32[48,128]{1,0:T(8,128)} %membrane_ref.1, s32[1,128]{1,0:T(1,128)} %bitcast.8, ...), custom_call_target="tpu_custom_call" | custom-call | tf_op jit(solution)/shard_map/cortex_window/pallas_call | solution.py:236
  45.1 1.4 %hand_over.1 = (f32[48,128]{1,0:T(8,128)}, f32[10,32]{1,0:T(8,128)}) custom-call(f32[48,128]{1,0:T(8,128)} %get-tuple-element.4.voltage_in, f32[10,32]{1,0:T(8,128)} %get-tuple-element.5.rates_in), custom_call_target="tpu_custom_call" | custom-call | tf_op jit(solution)/shard_map/hand_over/pallas_call | solution.py:273
